TPU v7x, 16 devices: a whole 2x2x2 slice. The times are simulated.
16 devices in a mesh: rep: 1, dp: 16 (over x, y, z, core).
Axes of the slice: x: 2, y: 2, z: 2, core: 2. Of those that a mesh axis runs over, the one named last changes fastest.
Arguments:
- a: bfloat16 [16, 4, 4096, 640], P(('rep', 'dp'))
- g: bfloat16 [16, 4, 4096, 4096], P(('rep', 'dp'))
Outputs:
- output: bfloat16 [4, 640, 4096], P('rep')
All inputs are finite; a program needn't handle non-finite values.
Results may differ from a plain program's by a relative error of at most 0.012.
Values are sent between devices in bfloat16 or wider.
A program may use at most 2 GiB of HBM per device.

v0:
```python
import jax
import jax.numpy as jnp


def solution(mesh):
    groups = mesh.shape["rep"]

    def step(a, g):
        a, g = (t.reshape(groups, -1, *t.shape[1:]) for t in (a, g))
        sums = jnp.einsum("rsntd,rsntf->rndf", a, g, preferred_element_type=jnp.float32)
        return sums.astype(jnp.bfloat16).reshape(-1, *sums.shape[2:])

    return step
```

profile of v0, /device:TPU:0, one launch (start us, length us, event | category | flops | bytes accessed | tf_op | source)
XLA Modules:
  0.0 484.1 jit_solution(14958419020964587525)
XLA Ops:
  0.0 97.8 %fusion = f32[4,640,4096]{2,1,0:T(8,128)} fusion(bf16[1,4,4096,4096]{3,2,1,0:T(8,128)(2,1)} %param.1, bf16[1,4,4096,640]{3,2,1,0:T(8,128)(2,1)} %param), kind=kOutput, calls=%fused_computation | convolution fusion | flops 85899345920 | bytes 197132288 | tf_op jit(solution)/rsntd,rsntf->rndf/dot_general | solution.py:10
  97.8 386.2 %all-reduce.2 = bf16[4,640,4096]{2,1,0:T(8,128)(2,1)} all-reduce(f32[4,640,4096]{2,1,0:T(8,128)} %fusion), channel_id=1, replica_groups=mesh['axis_0'=16] {'axis_0'}, use_global_device_ids=true, to_apply=%add.clone | all-reduce | flops 10485760 | bytes 62914560 | tf_op jit(solution)/rsntd,rsntf->rndf/dot_general | solution.py:10
where the time goes:
time: 484 us
  blocking collectives  386 us (80%)
  matrix products  97.8 us (20%)
    dot_general x1, blocking collectives, step(): jnp.einsum('rsntd,rsntf->rndf', a, g, preferred_element_type=jnp.float32)  386 us
    dot_general x1, matrix products, step(): jnp.einsum('rsntd,rsntf->rndf', a, g, preferred_element_type=jnp.float32)  97.8 us

commit v1 on v0

v1 whole, which is shorter than its diff:
```python
import functools

import jax
import jax.numpy as jnp
from jax import lax
from jax.experimental import pallas as pl
from jax.experimental.pallas import tpu as pltpu

MESH = pl.DeviceIdType.MESH
F32 = jnp.float32
BF16 = jnp.bfloat16

W = 512
UW = 256
KBLOCKS = 8
GSLOTS = 3
SLOTS = 8
LAGS = (2, 4, 8, 12, 16, 20)


def kernel(a_ref, g_ref, o_ref, at, stage, gbuf, acc, keep0, keep1, keep2,
           sbuf0, sbuf1, sbuf2, sbuf3, stage_sem, g_sem, send_sem, recv_sem, free_sem):
    matrices, tokens, d = a_ref.shape[1:]
    f = g_ref.shape[3]
    kb = tokens // KBLOCKS
    per = f // W
    chunks = matrices * per
    units = chunks * (W // UW)
    uper = f // UW

    me = lax.axis_index("dp")
    core = lax.rem(me, 2)
    z = lax.rem(me // 2, 2)
    y = lax.rem(me // 4, 2)
    x = lax.rem(me // 8, 2)
    other = me + 1 - 2 * core

    def bit_of(dim):
        return jnp.where(dim == 0, x, jnp.where(dim == 1, y, z))

    def peer_of(dim):
        b = bit_of(dim)
        step = jnp.where(dim == 0, 8, jnp.where(dim == 1, 4, 2))
        return me + step * (1 - 2 * b)

    def dims(u):
        r = lax.rem(u, 3)
        return r, lax.rem(r + 1, 3), lax.rem(r + 2, 3)

    def rows(u):
        d0, d1, d2 = dims(u)
        h1, h2, h3 = d // 2, d // 4, d // 8
        b0, b1, b2 = bit_of(d0), bit_of(d1), bit_of(d2)
        k1, s1 = b0 * h1, (1 - b0) * h1
        k2, s2 = k1 + b1 * h2, k1 + (1 - b1) * h2
        k3, s3 = k2 + b2 * h3, k2 + (1 - b2) * h3
        return (k1, k2, k3), (s1, s2, s3)

    def rds(start, size):
        return pl.ds(pl.multiple_of(start, 16), size)

    def cols(u, c):
        return pl.ds(pl.multiple_of(lax.rem(u, uper) * UW + c * 128, 128), 128)

    def mine(u):
        return u // uper, cols(u, core)

    def theirs(u):
        return u // uper, cols(u, 1 - core)

    def remote(src, dst, stage_no, u, device):
        return pltpu.make_async_remote_copy(
            src, dst, send_sem.at[stage_no, u], recv_sem.at[stage_no, u],
            device_id={"dp": device}, device_id_type=MESH)

    h1, h2, h3 = d // 2, d // 4, d // 8

    def core_reduce(u):
        n, c = mine(u)
        no, co = theirs(u)
        return remote(sbuf0.at[lax.rem(u, SLOTS)], o_ref.at[no, :, co], 0, u, other)

    def chip_reduce(u, s):
        n, c = theirs(u)
        dim = dims(u)[s]
        buf = (sbuf1, sbuf2, sbuf3)[s]
        start, size = ((0, h1), (h1, h2), (h1 + h2, h3))[s]
        return remote(buf.at[lax.rem(u, SLOTS)], o_ref.at[n, pl.ds(start, size), c], 1 + s, u, peer_of(dim))

    def chip_gather(u, s):
        n, c = mine(u)
        dim = dims(u)[2 - s]
        start = rows(u)[0][2 - s]
        size = (h3, h2, h1)[s]
        ref = o_ref.at[n, rds(start, size), c]
        return remote(ref, ref, 4 + s, u, peer_of(dim))

    def core_gather(u):
        n, c = mine(u)
        ref = o_ref.at[n, :, c]
        return remote(ref, ref, 7, u, other)

    def landed(ref, stage_no, u):
        pltpu.make_async_copy(ref, ref, recv_sem.at[stage_no, u]).wait()

    def left(ref, stage_no, u):
        pltpu.make_async_copy(ref, ref, send_sem.at[stage_no, u]).wait()

    def g_copy(j):
        n = j // per
        c = pl.ds(pl.multiple_of(lax.rem(j, per) * W, W), W)
        slot = lax.rem(j, GSLOTS)
        return pltpu.make_async_copy(g_ref.at[0, n, :, c], gbuf.at[slot], g_sem.at[slot])

    def a_copy(n, k):
        return pltpu.make_async_copy(
            a_ref.at[0, n, pl.ds(pl.multiple_of(k * kb, kb), kb), :], stage.at[k], stage_sem.at[k])

    def turn(n, k):
        at[lax.rem(n, 2), :, pl.ds(pl.multiple_of(k * kb, kb), kb)] = stage[k].T

    barrier = pltpu.get_barrier_semaphore()
    peers = [other] + [peer_of(i) for i in range(3)]
    for p in peers:
        pl.semaphore_signal(barrier, inc=1, device_id={"dp": p}, device_id_type=MESH)
    pl.semaphore_wait(barrier, len(peers))

    for k in range(KBLOCKS):
        a_copy(0, k).start()
    g_copy(0).start()
    g_copy(1).start()
    for k in range(KBLOCKS):
        a_copy(0, k).wait()
        turn(0, k)

    def matmul(j):
        n = j // per
        k = lax.rem(j, per)

        @pl.when(j + 2 < chunks)
        def _():
            g_copy(j + 2).start()

        more = n + 1 < matrices

        @pl.when(more & (k == 0))
        def _():
            for i in range(KBLOCKS):
                a_copy(n + 1, i).start()

        g_copy(j).wait()
        slot = lax.rem(j, 4)
        acc[slot] = jnp.dot(at[lax.rem(n, 2)], gbuf[lax.rem(j, GSLOTS)], preferred_element_type=F32)

        for i in range(W // UW):
            u = j * (W // UW) + i

            @pl.when(u >= SLOTS)
            def _():
                core_reduce(u - SLOTS).wait_send()

            c = pl.ds(pl.multiple_of(i * UW + (1 - core) * 128, 128), 128)
            sbuf0[lax.rem(u, SLOTS)] = acc[slot, :, c].astype(BF16)
            core_reduce(u).start()

        @pl.when(more)
        def _():
            a_copy(n + 1, k).wait()
            turn(n + 1, k)

    def halve(u, s, value):
        (k1, k2, k3), (s1, s2, s3) = rows(u)
        slot = lax.rem(u, SLOTS)

        @pl.when(u >= SLOTS)
        def _():
            chip_reduce(u - SLOTS, s).wait_send()

        buf = (sbuf1, sbuf2, sbuf3)[s]
        keep = (keep0, keep1, keep2)[s]
        size = (h1, h2, h3)[s]
        b = bit_of(dims(u)[s])
        buf[slot] = value((1 - b) * size, size).astype(BF16)
        chip_reduce(u, s).start()
        keep[slot] = value(b * size, size)

    def step1(u):
        core_reduce(u).wait_recv()
        n, c = mine(u)
        aslot = lax.rem(u // 2, 4)
        ac = pl.ds(pl.multiple_of(lax.rem(u, 2) * UW + core * 128, 128), 128)

        def value(start, size):
            return acc[aslot, rds(start, size), ac] + o_ref[n, rds(start, size), c].astype(F32)

        halve(u, 0, value)

    def step23(u, s):
        chip_reduce(u, s - 1).wait_recv()
        n, c = theirs(u)
        slot = lax.rem(u, SLOTS)
        keep = (keep0, keep1)[s - 1]
        base = (0, h1)[s - 1]

        def value(start, size):
            return keep[slot, rds(start, size), :] + o_ref[n, rds(base + start, size), c].astype(F32)

        halve(u, s, value)

    def step4(u):
        chip_reduce(u, 2).wait_recv()
        n, c = theirs(u)
        slot = lax.rem(u, SLOTS)
        total = keep2[slot] + o_ref[n, pl.ds(h1 + h2, h3), c].astype(F32)
        n, c = mine(u)
        o_ref[n, rds(rows(u)[0][2], h3), c] = total.astype(BF16)
        chip_gather(u, 0).start()
        pl.semaphore_signal(free_sem, inc=1, device_id={"dp": other}, device_id_type=MESH)

    def step5(u):
        chip_gather(u, 0).wait_recv()
        chip_gather(u, 1).start()

    def step6(u):
        chip_gather(u, 1).wait_recv()
        chip_gather(u, 2).start()

    def step7(u):
        chip_gather(u, 2).wait_recv()
        pl.semaphore_wait(free_sem, 1)
        core_gather(u).start()

    steps = (step1, lambda u: step23(u, 1), lambda u: step23(u, 2), step4, step5)

    def slot(t, _):
        @pl.when(t < chunks)
        def _():
            matmul(t)

        for lag, step in zip(LAGS, steps):
            for i in range(2):
                u = 2 * t + i - lag

                @pl.when((u >= 0) & (u < units))
                def _():
                    step(u)
        lo, hi = sched6(t), sched6(t + 1)
        lax.fori_loop(lo, hi, lambda u, _: (step6(u), 0)[1], 0)
        lo, hi = sched7(t), sched7(t + 1)
        lax.fori_loop(lo, hi, lambda u, _: (step7(u), 0)[1], 0)
        return 0

    def clip(v):
        return jnp.minimum(jnp.maximum(v, 0), units)

    def sched6(t):
        return clip(2 * t - LAGS[5])

    def sched7(t):
        return clip(2 * t - LAGS[5] - 6)

    slots = (units + LAGS[5] + 6) // 2
    lax.fori_loop(0, slots, slot, 0)

    def finish(u, _):
        core_gather(u).wait_send()
        core_gather(u).wait_recv()
        for s in range(3):
            chip_gather(u, s).wait_send()
        return 0

    lax.fori_loop(0, units, finish, 0)

    def drain(u, _):
        core_reduce(u).wait_send()
        for s in range(3):
            chip_reduce(u, s).wait_send()
        return 0

    lax.fori_loop(units - SLOTS, units, drain, 0)


def solution(mesh):
    def body(a, g):
        _, n, tokens, d = a.shape
        f = g.shape[3]
        units = n * f // UW
        return pl.pallas_call(
            kernel,
            out_shape=pltpu.VMEM((n, d, f), BF16),
            in_specs=[pl.BlockSpec(memory_space=pl.ANY)] * 2,
            out_specs=pl.BlockSpec(memory_space=pltpu.VMEM),
            scratch_shapes=[
                pltpu.VMEM((2, d, tokens), BF16),
                pltpu.VMEM((KBLOCKS, tokens // KBLOCKS, d), BF16),
                pltpu.VMEM((GSLOTS, tokens, W), BF16),
                pltpu.VMEM((4, d, W), F32),
                pltpu.VMEM((SLOTS, d // 2, 128), F32),
                pltpu.VMEM((SLOTS, d // 4, 128), F32),
                pltpu.VMEM((SLOTS, d // 8, 128), F32),
                pltpu.VMEM((SLOTS, d, 128), BF16),
                pltpu.VMEM((SLOTS, d // 2, 128), BF16),
                pltpu.VMEM((SLOTS, d // 4, 128), BF16),
                pltpu.VMEM((SLOTS, d // 8, 128), BF16),
                pltpu.SemaphoreType.DMA((KBLOCKS,)),
                pltpu.SemaphoreType.DMA((GSLOTS,)),
                pltpu.SemaphoreType.DMA((8, units)),
                pltpu.SemaphoreType.DMA((8, units)),
                pltpu.SemaphoreType.REGULAR,
            ],
            compiler_params=pltpu.CompilerParams(
                collective_id=0, has_side_effects=True, vmem_limit_bytes=43 * 2**20),
        )(a, g)

    spec = jax.sharding.PartitionSpec
    return jax.shard_map(
        body, mesh=mesh, in_specs=(spec(("rep", "dp")), spec(("rep", "dp"))), out_specs=spec("rep"), check_vma=False)
```

time: 484 us -> 188 us (0.39)
  blocking collectives: 386 us -> 0 us
  Pallas kernels: 0 us -> 180 us
  matrix products: 97.8 us -> 0 us
  local copies, waits for them, and re-layouts: 0 us -> 7.54 us
    dot_general x1 -> x0, blocking collectives: 386 us -> none  [step(): jnp.einsum('rsntd,rsntf->rndf', a, g, preferred_element_type=jnp.float32)]
    pallas_call x0 -> x1, Pallas kernels: none -> 180 us  [body(): pl.pallas_call(kernel, out_shape=pltpu.VMEM((n, d, f), BF16), in_specs=[p...]
    dot_general x1 -> x0, matrix products: 97.8 us -> none  [step(): jnp.einsum('rsntd,rsntf->rndf', a, g, preferred_element_type=jnp.float32)]
    unnamed x0 -> x1, local copies, waits for them, and re-layouts: none -> 7.54 us
where the time goes in v1:
time: 188 us
  Pallas kernels  180 us (96%)
  local copies, waits for them, and re-layouts  7.54 us (4%)
    pallas_call x1, Pallas kernels, body(): pl.pallas_call(kernel, out_shape=pltpu.VMEM((n, d, f), BF16), in_specs=[p...  180 us
    unnamed x1, local copies, waits for them, and re-layouts  7.54 us

profile of v1, /device:TPU:0, one launch (start us, length us, event | category | flops | bytes accessed | tf_op | source)
XLA Modules:
  0.0 188.0 jit_solution(2953602796359217547)
XLA Ops:
  0.0 180.4 %shard_map.28 = bf16[4,640,4096]{2,1,0:T(8,128)(2,1)S(1)} custom-call(bf16[1,4,4096,640]{3,2,1,0:T(8,128)(2,1)} %a_ref.1, bf16[1,4,4096,4096]{3,2,1,0:T(8,128)(2,1)} %g_ref.1), custom_call_target="tpu_custom_call" | custom-call | tf_op jit(solution)/shard_map/pallas_call | solution.py:288
  180.4 7.5 %copy.4 = bf16[4,640,4096]{2,1,0:T(8,128)(2,1)} copy(bf16[4,640,4096]{2,1,0:T(8,128)(2,1)S(1)} %shard_map.28) | data formatting | bytes 41943040

commit v2 on v1

--- a/solution.py
+++ b/solution.py
@@ -11,11 +11,11 @@
 BF16 = jnp.bfloat16
 
 W = 512
-UW = 256
+UW = 512
 KBLOCKS = 8
 GSLOTS = 3
-SLOTS = 8
-LAGS = (2, 4, 8, 12, 16, 20)
+SLOTS = 4
+LAGS = (1, 3, 5, 7, 9, 11)
 
 
 def kernel(a_ref, g_ref, o_ref, at, stage, gbuf, acc, keep0, keep1, keep2,
@@ -60,7 +60,7 @@
         return pl.ds(pl.multiple_of(start, 16), size)
 
     def cols(u, c):
-        return pl.ds(pl.multiple_of(lax.rem(u, uper) * UW + c * 128, 128), 128)
+        return pl.ds(pl.multiple_of(lax.rem(u, uper) * UW + c * 256, 256), 256)
 
     def mine(u):
         return u // uper, cols(u, core)
@@ -159,7 +159,7 @@
             def _():
                 core_reduce(u - SLOTS).wait_send()
 
-            c = pl.ds(pl.multiple_of(i * UW + (1 - core) * 128, 128), 128)
+            c = pl.ds(pl.multiple_of(i * UW + (1 - core) * 256, 256), 256)
             sbuf0[lax.rem(u, SLOTS)] = acc[slot, :, c].astype(BF16)
             core_reduce(u).start()
 
@@ -187,8 +187,8 @@
     def step1(u):
         core_reduce(u).wait_recv()
         n, c = mine(u)
-        aslot = lax.rem(u // 2, 4)
-        ac = pl.ds(pl.multiple_of(lax.rem(u, 2) * UW + core * 128, 128), 128)
+        aslot = lax.rem(u, 4)
+        ac = pl.ds(pl.multiple_of(core * 256, 256), 256)
 
         def value(start, size):
             return acc[aslot, rds(start, size), ac] + o_ref[n, rds(start, size), c].astype(F32)
@@ -238,8 +238,8 @@
             matmul(t)
 
         for lag, step in zip(LAGS, steps):
-            for i in range(2):
-                u = 2 * t + i - lag
+            for i in range(1):
+                u = t - lag
 
                 @pl.when((u >= 0) & (u < units))
                 def _():
@@ -254,12 +254,12 @@
         return jnp.minimum(jnp.maximum(v, 0), units)
 
     def sched6(t):
-        return clip(2 * t - LAGS[5])
+        return clip(t - LAGS[5])
 
     def sched7(t):
-        return clip(2 * t - LAGS[5] - 6)
-
-    slots = (units + LAGS[5] + 6) // 2
+        return clip(t - LAGS[5] - 4)
+
+    slots = units + LAGS[5] + 4
     lax.fori_loop(0, slots, slot, 0)
 
     def finish(u, _):
@@ -295,13 +295,13 @@
                 pltpu.VMEM((KBLOCKS, tokens // KBLOCKS, d), BF16),
                 pltpu.VMEM((GSLOTS, tokens, W), BF16),
                 pltpu.VMEM((4, d, W), F32),
-                pltpu.VMEM((SLOTS, d // 2, 128), F32),
-                pltpu.VMEM((SLOTS, d // 4, 128), F32),
-                pltpu.VMEM((SLOTS, d // 8, 128), F32),
-                pltpu.VMEM((SLOTS, d, 128), BF16),
-                pltpu.VMEM((SLOTS, d // 2, 128), BF16),
-                pltpu.VMEM((SLOTS, d // 4, 128), BF16),
-                pltpu.VMEM((SLOTS, d // 8, 128), BF16),
+                pltpu.VMEM((SLOTS, d // 2, 256), F32),
+                pltpu.VMEM((SLOTS, d // 4, 256), F32),
+                pltpu.VMEM((SLOTS, d // 8, 256), F32),
+                pltpu.VMEM((SLOTS, d, 256), BF16),
+                pltpu.VMEM((SLOTS, d // 2, 256), BF16),
+                pltpu.VMEM((SLOTS, d // 4, 256), BF16),
+                pltpu.VMEM((SLOTS, d // 8, 256), BF16),
                 pltpu.SemaphoreType.DMA((KBLOCKS,)),
                 pltpu.SemaphoreType.DMA((GSLOTS,)),
                 pltpu.SemaphoreType.DMA((8, units)),

time: 188 us -> 179 us (0.952)
  Pallas kernels: 180 us -> 171 us
    pallas_call x1, Pallas kernels: 180 us -> 171 us  [body(): pl.pallas_call(kernel, out_shape=pltpu.VMEM((n, d, f), BF16), in_specs=[p...]
where the time goes in v2:
time: 179 us
  Pallas kernels  171 us (96%)
  local copies, waits for them, and re-layouts  7.54 us (4%)
    pallas_call x1, Pallas kernels, body(): pl.pallas_call(kernel, out_shape=pltpu.VMEM((n, d, f), BF16), in_specs=[p...  171 us
    unnamed x1, local copies, waits for them, and re-layouts  7.54 us

profile of v2, /device:TPU:0, one launch (start us, length us, event | category | flops | bytes accessed | tf_op | source)
XLA Modules:
  0.0 178.7 jit_solution(2505827504297858135)
XLA Ops:
  0.0 171.2 %shard_map.28 = bf16[4,640,4096]{2,1,0:T(8,128)(2,1)S(1)} custom-call(bf16[1,4,4096,640]{3,2,1,0:T(8,128)(2,1)} %a_ref.1, bf16[1,4,4096,4096]{3,2,1,0:T(8,128)(2,1)} %g_ref.1), custom_call_target="tpu_custom_call" | custom-call | tf_op jit(solution)/shard_map/pallas_call | solution.py:288
  171.2 7.5 %copy.4 = bf16[4,640,4096]{2,1,0:T(8,128)(2,1)} copy(bf16[4,640,4096]{2,1,0:T(8,128)(2,1)S(1)} %shard_map.28) | data formatting | bytes 41943040
